TPU v7x, 32 devices: a 4x4x1 block of a 4x4x8 slice. The times are simulated.
32 devices in a mesh: dp: 1 (over z), tp: 4 (over y), sp: 8 (over x, core).
Axes of the slice: x: 4, y: 4, z: 1, core: 2. Of those that a mesh axis runs over, the one named last changes fastest.
The devices are a block of a 4x4x8 slice.
Arguments:
- hidden: bfloat16 [16, 4096], P('dp')
- k_cache: bfloat16 [16, 4096, 32, 128], P('dp', 'sp', 'tp')
- v_cache: bfloat16 [16, 4096, 32, 128], P('dp', 'sp', 'tp')
- lengths: int32 [16], P('dp')
- rel_table: bfloat16 [4096, 32, 128], P('sp', 'tp')
- u_bias: bfloat16 [32, 128], P('tp')
- w_bias: bfloat16 [32, 128], P('tp')
- g_attn: bfloat16 [4096], replicated
- w_query: bfloat16 [4096, 32, 128], P(None, 'tp')
- w_key: bfloat16 [4096, 32, 128], P(None, 'tp')
- w_value: bfloat16 [4096, 32, 128], P(None, 'tp')
- w_out: bfloat16 [32, 128, 4096], P('tp')
- g_mlp: bfloat16 [4096], replicated
- w_up: bfloat16 [4096, 16384], P(None, 'tp')
- w_down: bfloat16 [16384, 4096], P('tp')
Outputs:
- output: bfloat16 [16, 4096], P('dp')
All inputs are finite; a program needn't handle non-finite values.
Results may differ from a plain program's by a relative error of at most 0.014473.
Values sent between devices are 32-bit elements.
A program may use at most 768 MiB of HBM per device.

v0:
```python
import jax
import jax.numpy as jnp
from jax import lax
from jax.sharding import PartitionSpec as P

EPS = 1e-6
MASKED = -1e30


def rms_norm(tensor, gain):
    wide = tensor.astype(jnp.float32)
    mean_sq = jnp.mean(wide * wide, axis=-1, keepdims=True)
    return (wide * lax.rsqrt(mean_sq + EPS) * gain.astype(jnp.float32)).astype(jnp.bfloat16)


def distance_to_position(by_distance, first_pos, lengths, width):
    padded = jnp.pad(by_distance, ((0, 0), (0, 0), (width, 0)))
    starts = lengths - first_pos + 1
    taken = jax.vmap(lambda row, begin: lax.dynamic_slice_in_dim(row, begin, width, axis=1))(padded, starts)
    return jnp.flip(taken, axis=2)


def solution(mesh):
    spec_rows = P('dp', None)
    spec_cache = P('dp', 'sp', 'tp', None)
    in_specs = (spec_rows, spec_cache, spec_cache, P('dp'), P('sp', 'tp', None), P('tp', None), P('tp', None), P(None), P(None, 'tp', None), P(None, 'tp', None), P(None, 'tp', None), P('tp', None, None), P(None), P(None, 'tp'), P('tp', None))
    out_specs = spec_rows

    def layer_step(hidden, k_cache, v_cache, lengths, rel_table, u_bias, w_bias, g_attn, w_query, w_key, w_value, w_out, g_mlp, w_up, w_down):
        seq_blk = k_cache.shape[1]
        head_dim = k_cache.shape[3]
        first_pos = lax.axis_index('sp') * seq_blk
        normed = rms_norm(hidden, g_attn)
        query_vec = jnp.einsum('do,ojf->djf', normed, w_query, preferred_element_type=jnp.float32).astype(jnp.bfloat16)
        key_new = jnp.einsum('do,ojf->djf', normed, w_key, preferred_element_type=jnp.float32).astype(jnp.bfloat16)
        value_new = jnp.einsum('do,ojf->djf', normed, w_value, preferred_element_type=jnp.float32).astype(jnp.bfloat16)
        positions = first_pos + jnp.arange(seq_blk)
        write_mask = (positions[None, :] == lengths[:, None])[:, :, None, None]
        k_updated = jnp.where(write_mask, key_new[:, None], k_cache)
        v_updated = jnp.where(write_mask, value_new[:, None], v_cache)
        q_content = (query_vec.astype(jnp.float32) + u_bias.astype(jnp.float32)).astype(jnp.bfloat16)
        q_position = (query_vec.astype(jnp.float32) + w_bias.astype(jnp.float32)).astype(jnp.bfloat16)
        content = jnp.einsum('bhd,bshd->bhs', q_content, k_updated, preferred_element_type=jnp.float32)
        rel_local = jnp.einsum('bhd,shd->bhs', q_position, rel_table, preferred_element_type=jnp.float32)
        rel_all = lax.all_gather(rel_local, 'sp', axis=2, tiled=True)
        relative = distance_to_position(rel_all, first_pos, lengths, seq_blk)
        valid = (positions[None, :] <= lengths[:, None])[:, None, :]
        scores = jnp.where(valid, (content + relative) * (head_dim ** -0.5), MASKED)
        local_max = jnp.max(scores, axis=2)
        weights = jnp.where(valid, jnp.exp(scores - local_max[:, :, None]), 0.0)
        local_sum = jnp.sum(weights, axis=2)
        partial_ctx = jnp.einsum('bhs,bshd->bhd', weights.astype(jnp.bfloat16), v_updated, preferred_element_type=jnp.float32)
        packed = jnp.concatenate([partial_ctx, local_max[:, :, None], local_sum[:, :, None]], axis=2)
        gathered = lax.all_gather(packed, 'sp', axis=0)
        block_ctx = gathered[:, :, :, :head_dim]
        block_max = gathered[:, :, :, head_dim]
        block_sum = gathered[:, :, :, head_dim + 1]
        global_max = jnp.max(block_max, axis=0)
        rescale = jnp.exp(block_max - global_max[None])
        total = jnp.sum(rescale * block_sum, axis=0)
        context = (jnp.sum(rescale[:, :, :, None] * block_ctx, axis=0) / total[:, :, None]).astype(jnp.bfloat16)
        attn_part = jnp.einsum('bhd,hdm->bm', context, w_out, preferred_element_type=jnp.float32)
        attn_out = lax.psum(attn_part, 'tp')
        resid_mid = (hidden.astype(jnp.float32) + attn_out).astype(jnp.bfloat16)
        normed_mlp = rms_norm(resid_mid, g_mlp)
        up_proj = jnp.dot(normed_mlp, w_up, preferred_element_type=jnp.float32)
        activated = jax.nn.gelu(up_proj, approximate=True).astype(jnp.bfloat16)
        down_part = jnp.dot(activated, w_down, preferred_element_type=jnp.float32)
        down_proj = lax.psum(down_part, 'tp')
        hidden_out = (resid_mid.astype(jnp.float32) + down_proj).astype(jnp.bfloat16)
        return hidden_out

    return jax.shard_map(layer_step, mesh=mesh, in_specs=in_specs, out_specs=out_specs, check_vma=False)
```

profile of v0, /device:TPU:97, one launch (start us, length us, event | category | flops | bytes accessed | tf_op | source)
XLA Modules:
  0.0 288.4 jit_solution(3288765273930089916)
XLA Ops:
  6.5 0.0 copy-start
  6.6 0.0 copy-start.4
  6.6 0.0 all-gather.3.cloned.1.call-start
  6.6 0.8 convert_element_type.67
  7.3 0.7 convert_element_type.63
  8.0 1.0 fusion.27
  9.1 0.7 convert_element_type.70
  9.8 4.7 %fusion.60 = (f32[16,8,128]{2,0,1:T(8,128)S(1)}, f32[16,8,128]{2,0,1:T(8,128)S(1)}) fusion(f32[8,128]{1,0:T(8,128)S(1)} %convert_element_type.67, bf16[4096,8,128]{2,1,0:T(8,128)(2,1)} %param.23, bf16[16,4096]{1,0:T(8,128)(2,1)} %param.15, f32[4096]{0:T(1024)S(1)} %convert_element_type.63, f32[16]{0:T(128)S(1)} %add_rsqrt_fusion.1), kind=kOutput, calls=%fused_computation.63 | convolution fusion | flops 134561792 | bytes 8671296 | tf_op jit(solution)/shard_map/do,ojf->djf/dot_general | solution.py:34
  14.5 0.0 copy-done
  14.5 1.1 convolution_bitcast_fusion.1
  15.6 0.1 all-gather.3.cloned.1.call-update
  15.7 0.1 all-reduce.5.cloned.1.call-start
  15.8 0.0 copy-done.4
  15.8 0.0 copy-start.6
  15.8 4.6 %fusion.19 = bf16[16,8,128]{2,0,1:T(8,128)(2,1)S(1)} fusion(bf16[4096,8,128]{2,1,0:T(8,128)(2,1)} %param.24, bf16[16,4096]{1,0:T(8,128)(2,1)S(1)} %copy-done.4, f32[4096]{0:T(1024)S(1)} %convert_element_type.63, f32[16]{0:T(128)S(1)} %add_rsqrt_fusion.1), kind=kOutput, calls=%fused_computation.22 | convolution fusion | flops 134496256 | bytes 8568896 | tf_op jit(solution)/shard_map/do,ojf->djf/dot_general | solution.py:35
  20.4 4.6 %fusion.22 = bf16[16,8,128]{2,0,1:T(8,128)(2,1)S(1)} fusion(bf16[4096,8,128]{2,1,0:T(8,128)(2,1)} %param.25, bf16[16,4096]{1,0:T(8,128)(2,1)S(1)} %copy-done.4, f32[4096]{0:T(1024)S(1)} %convert_element_type.63, f32[16]{0:T(128)S(1)} %add_rsqrt_fusion.1), kind=kOutput, calls=%fused_computation.23 | convolution fusion | flops 134496256 | bytes 8568896 | tf_op jit(solution)/shard_map/do,ojf->djf/dot_general | solution.py:36
  25.1 0.0 copy-done.6
  25.1 0.1 broadcast_compare_fusion.1
  25.2 0.2 copy.97
  25.4 29.0 %multiply_reduce_fusion = f32[16,8,512]{1,2,0:T(8,128)} fusion(f32[16,8,128]{2,1,0:T(8,128)S(1)} %copy.129, bf16[16,512,8,128]{3,2,1,0:T(8,128)(2,1)} %param.16, pred[16,512]{1,0:T(8,128)(4,1)S(1)} %get-tuple-element.13, bf16[16,8,128]{2,1,0:T(8,128)(2,1)S(1)} %copy.100), kind=kLoop, calls=%fused_computation.1 | loop fusion | flops 33488896 | bytes 17145856
  54.4 13.6 %broadcast_select_fusion = bf16[16,512,8,128]{3,2,1,0:T(8,128)(2,1)} fusion(bf16[16,512,8,128]{3,2,1,0:T(8,128)(2,1)} %param.17, pred[16,512]{1,0:T(8,128)(4,1)S(1)} %get-tuple-element.13, bf16[16,8,128]{2,1,0:T(8,128)(2,1)S(1)} %copy.104), kind=kLoop, calls=%fused_computation.4 | loop fusion | flops 8388608 | bytes 33595392 | tf_op jit(solution)/shard_map/jit(_where)/select_n | solution.py:40
  68.0 0.0 all-gather.3.cloned.1.call-done
  68.0 17.5 %copy.130 = f32[16,8,4096]{1,0,2:T(8,128)} copy(f32[16,8,4096]{2,0,1:T(8,128)} %all-gather.3.cloned.1.call-done) | data formatting | bytes 4194304
  85.5 25.2 %pad.5.clone = f32[16,8,4608]{1,0,2:T(8,128)} pad(f32[16,8,4096]{1,0,2:T(8,128)} %copy.130, f32[]{:T(128)} %constant.17.clone.1), padding=0_0x0_0x512_0 | pad | bytes 4456452 | tf_op jit(solution)/shard_map/jit(_pad)/pad | solution.py:17
  110.7 7.8 %gather_fusion = f32[16,8,512]{1,0,2:T(8,128)} fusion(f32[16,8,4608]{1,0,2:T(8,128)} %pad.5.clone, s32[16]{0:T(128)S(1)} %fusion.66), kind=kCustom, calls=%fused_computation | custom fusion | bytes 524480 | tf_op jit(solution)/shard_map/vmap()/gather | solution.py:19
  118.5 0.0 copy-start.2
  118.5 0.0 copy-start.3
  118.5 8.1 %fusion.74 = f32[16,8]{1,0:T(8,128)S(1)} fusion(f32[16,8,512]{1,0,2:T(8,128)} %gather_fusion, f32[16,8,512]{1,2,0:T(8,128)} %multiply_reduce_fusion, pred[16,512]{0,1:T(8,128)(4,1)S(1)} %copy.97), kind=kLoop, calls=%fused_computation.85 | loop fusion | flops 262016 | bytes 532992 | tf_op jit(solution)/shard_map/reduce_max | solution.py:49
  126.6 0.0 copy-done.2
  126.6 0.0 copy-done.3
  126.6 10.4 %fusion.12 = (bf16[16,8,512,1]{1,0,2,3:T(8,128)(2,1)S(1)}, f32[16,8]{1,0:T(8,128)S(1)}) fusion(f32[16,8]{1,0:T(8,128)S(1)} %fusion.74, pred[16,512]{0,1:T(8,128)(4,1)S(1)} %copy.97, f32[16,8,512]{1,0,2:T(8,128)S(1)} %copy-done.3, f32[16,8,512]{1,2,0:T(8,128)S(1)} %copy-done.2), kind=kLoop, calls=%fused_computation.18 | loop fusion | flops 458624 | bytes 664576 | tf_op jit(solution)/shard_map/convert_element_type | solution.py:52
  137.0 0.2 copy.108
  137.2 0.2 copy.107
  137.4 1.9 copy.121
  139.3 8.1 %fusion = f32[16,8,1,128]{3,2,1,0:T(1,128)S(1)} fusion(bf16[16,8,512,1]{2,3,1,0:T(2,128)(2,1)S(1)} %copy.121, bf16[16,512,8,128]{3,2,1,0:T(8,128)(2,1)} %broadcast_select_fusion), kind=kOutput, calls=%fused_computation.2 | convolution fusion | flops 16777216 | bytes 16973824 | tf_op jit(solution)/shard_map/bhs,bshd->bhd/dot_general | solution.py:52
  147.4 0.0 copy-start.5
  147.4 0.1 pad_maximum_fusion
  147.5 21.7 %all-gather = f32[128,8,130]{2,1,0:T(8,128)S(1)} all-gather(f32[16,8,130]{2,1,0:T(8,128)S(1)} %pad_maximum_fusion), channel_id=2, replica_groups=mesh['dp'=1,'tp'=4,'sp'=8] {'sp'}, dimensions={0}, use_global_device_ids=true | all-gather | bytes 599040 | tf_op jit(solution)/shard_map/all_gather | solution.py:54
  169.2 0.3 fusion.76
  169.4 0.5 copy.128
  169.9 0.1 copy.132
  170.0 0.1 copy.110
  170.1 0.2 fusion.26
  170.3 0.5 copy.111
  170.8 0.1 copy.112
  170.8 0.1 divide_convert_fusion
  170.9 5.3 %convolution_bitcast_fusion = f32[16,4096]{1,0:T(8,128)} fusion(bf16[8,128,4096]{2,1,0:T(8,128)(2,1)} %param.26, bf16[16,8,128]{2,1,0:T(8,128)(2,1)S(1)} %divide_convert_fusion), kind=kOutput, calls=%fused_computation.11 | convolution fusion | flops 134217728 | bytes 8683520 | tf_op jit(solution)/shard_map/bhd,hdm->bm/dot_general | solution.py:62
  176.2 0.1 all-reduce.5.cloned.1.call-update
  176.3 0.1 all-reduce.7.cloned.1.call-start
  176.4 0.0 copy-done.5
  176.4 40.6 %all-reduce.5.cloned.1.call-done = f32[16,4096]{1,0:T(8,128)} async-done(((f32[16,4096]{1,0:T(8,128)}), f32[16,4096]{1,0:T(8,128)}) %all-reduce.5.cloned.1.call-update) | async-done | bytes 262160 | tf_op jit(solution)/shard_map/psum | solution.py:63
  217.0 1.1 fusion.31
  218.1 0.0 copy-start.1
  218.1 24.7 %fusion.43 = f32[16,4096]{1,0:T(8,128)} fusion(bf16[4096,4096]{1,0:T(8,128)(2,1)} %param.29, bf16[4096,4096]{1,0:T(8,128)(2,1)} %param.28, bf16[16,4096]{1,0:T(8,128)(2,1)S(1)} %get-tuple-element.6, f32[4096]{0:T(1024)S(1)} %convert_element_type.77, f32[16]{0:T(128)S(1)} %add_rsqrt_fusion), kind=kOutput, calls=%fused_computation.50 | convolution fusion | flops 1074593792 | bytes 67518528 | tf_op jit(solution)/shard_map/dot_general | solution.py:68
  242.8 0.1 all-reduce.7.cloned.1.call-update
  242.9 37.3 %all-reduce.7.cloned.1.call-done = f32[16,4096]{1,0:T(8,128)} async-done(((f32[16,4096]{1,0:T(8,128)}), f32[16,4096]{1,0:T(8,128)}) %all-reduce.7.cloned.1.call-update) | async-done | bytes 262160 | tf_op jit(solution)/shard_map/psum | solution.py:69
  280.2 1.6 fusion.34
  281.8 0.0 copy-done.1
  (10 shorter events, 0.1 us)
Async XLA Ops:
  6.5 7.9 %copy-start = (bf16[512,8,128]{2,1,0:T(8,128)(2,1)S(1)}, bf16[512,8,128]{2,1,0:T(8,128)(2,1)}, u32[]{:S(2)}) copy-start(bf16[512,8,128]{2,1,0:T(8,128)(2,1)} %param.19) | copy-start | bytes 3145732
  6.6 9.2 %copy-start.4 = (bf16[16,4096]{1,0:T(8,128)(2,1)S(1)}, bf16[16,4096]{1,0:T(8,128)(2,1)}, u32[]{:S(2)}) copy-start(bf16[16,4096]{1,0:T(8,128)(2,1)} %param.15) | copy-start | bytes 393220
  6.6 61.4 %all-gather.3.cloned.1.call-start = ((), (), s32[]{:S(2)}) async-start(), calls=%async_computation | async-start | bytes 2359296 | tf_op jit(solution)/shard_map/all_gather | solution.py:45
  15.7 201.3 %all-reduce.5.cloned.1.call-start = ((), (), s32[]{:S(2)}) async-start(), calls=%async_computation.1 | async-start | bytes 524288 | tf_op jit(solution)/shard_map/psum | solution.py:63
  15.8 9.3 %copy-start.6 = (s32[16]{0:T(128)S(1)}, s32[16]{0:T(128)}, u32[]{:S(2)}) copy-start(s32[16]{0:T(128)} %param.18) | copy-start | bytes 196
  118.5 8.1 %copy-start.2 = (f32[16,8,512]{1,2,0:T(8,128)S(1)}, f32[16,8,512]{1,2,0:T(8,128)}, u32[]{:S(2)}) copy-start(f32[16,8,512]{1,2,0:T(8,128)} %multiply_reduce_fusion) | copy-start | bytes 786436
  118.5 8.1 %copy-start.3 = (f32[16,8,512]{1,0,2:T(8,128)S(1)}, f32[16,8,512]{1,0,2:T(8,128)}, u32[]{:S(2)}) copy-start(f32[16,8,512]{1,0,2:T(8,128)} %gather_fusion) | copy-start | bytes 786436
  147.4 29.0 %copy-start.5 = (bf16[4096]{0:T(1024)(128)(2,1)S(1)}, bf16[4096]{0:T(1024)(128)(2,1)}, u32[]{:S(2)}) copy-start(bf16[4096]{0:T(1024)(128)(2,1)} %param.27) | copy-start | bytes 24580
  176.3 103.9 %all-reduce.7.cloned.1.call-start = ((), (), s32[]{:S(2)}) async-start(), calls=%async_computation.2 | async-start | bytes 524288 | tf_op jit(solution)/shard_map/psum | solution.py:69
  218.1 63.7 %copy-start.1 = (bf16[512,8,128]{2,1,0:T(8,128)(2,1)S(1)}, bf16[512,8,128]{2,1,0:T(8,128)(2,1)}, u32[]{:S(2)}) copy-start(bf16[512,8,128]{2,1,0:T(8,128)(2,1)} %param.19) | copy-start | bytes 3145732
Sparse Core Ops, SparseCore 0:
  15.8 26.8 all-gather.2
  176.4 40.5 all-reduce.4
  243.0 37.1 all-reduce.6
where the time goes:
time: 290 us; the launch traced here: 288 us
  waiting for transfers between devices  78.1 us (27%)
  other arithmetic  67.9 us (23%)
  local copies, waits for them, and re-layouts  54.1 us (19%)
  matrix products  53.1 us (18%)
  blocking collectives  21.7 us (7%)
  between operations  13.3 us (5%)
    psum x1, waiting for transfers between devices, layer_step(): attn_out = lax.psum(attn_part, 'tp')  40.6 us
    psum x1, waiting for transfers between devices, layer_step(): down_proj = lax.psum(down_part, 'tp')  37.3 us
    unnamed x1, other arithmetic  29 us
    pad x1, local copies, waits for them, and re-layouts, distance_to_position(): padded = jnp.pad(by_distance, ((0, 0), (0, 0), (width, 0)))  25.2 us
    dot_general x1, matrix products, layer_step(): down_part = jnp.dot(activated, w_down, preferred_element_type=jnp.float32)  24.7 us
    all_gather x1, blocking collectives, layer_step(): gathered = lax.all_gather(packed, 'sp', axis=0)  21.7 us
    unnamed x18, local copies, waits for them, and re-layouts  18.1 us
    select_n x1, other arithmetic, layer_step(): v_updated = jnp.where(write_mask, value_new[:, None], v_cache)  13.6 us
  transfers between devices with their start and end apart: 3, of which 2 were waited for; matrix products, arithmetic and copies ran while one was open for 18% of the time, Pallas kernels for 0%

commit v1 on v0

v1 whole, which is shorter than its diff:
```python
import functools

import jax
import jax.numpy as jnp
from jax import lax
from jax.experimental import pallas as pl
from jax.experimental.pallas import tpu as pltpu
from jax.sharding import PartitionSpec as P

EPS = 1e-6
MASKED = -1e30
FLOOR = -5e29
LANES = 128
F32 = jnp.float32
BF16 = jnp.bfloat16
NT = (((1,), (1,)), ((), ()))


def layer_kernel(n_sp, n_tp,
                 lens, hid, u_ref, w_ref, ga, gm, rel_hbm, k_hbm, v_hbm, wq_hbm, wk_hbm, wv_hbm, wo_hbm, wu_hbm, wd_hbm,
                 out_ref,
                 wqkv, relb, rrev, kb, vb, wob, wub, wdb,
                 qsend, qrecv, kvsend, kvrecv, qall, qcb, relsend, grid_rel, win, sc, csend, crecv, call, aosend, aorecv,
                 x1all, aall, dnsend, dnrecv, oall,
                 hsem, ssem, rsem, rel_ssem, rel_rsem, tp_ssem, tp_rsem):
    me = lax.axis_index('sp')
    my_tp = lax.axis_index('tp')
    batch = hid.shape[0]
    heads = u_ref.shape[0]
    head_dim = u_ref.shape[1]
    rows = kb.shape[1]
    seq_blk = rows // heads
    kk = wqkv.shape[1] // heads
    co = wob.shape[1]
    per_row = LANES // heads
    rel_rows = seq_blk // per_row
    smax = seq_blk * n_sp
    half = rows // 2
    scale = head_dim ** -0.5

    copies = []

    def fetch(src, dst):
        copy = pltpu.make_async_copy(src, dst, hsem.at[len(copies)])
        copies.append(copy)
        copy.start()
        return copy

    w_rows = pl.ds(pl.multiple_of(me * kk * heads, kk * heads), kk * heads)
    w_copies = [fetch(src.at[w_rows], wqkv.at[i]) for i, src in enumerate((wq_hbm, wk_hbm, wv_hbm))]
    rel_copy = fetch(rel_hbm, relb)
    k_copies = [fetch(k_hbm.at[b], kb.at[b]) for b in range(batch)]
    v_copies = [fetch(v_hbm.at[b], vb.at[b]) for b in range(batch)]
    o_cols = pl.ds(pl.multiple_of(me * co, co), co)
    wo_copy = fetch(wo_hbm.at[:, o_cols], wob)
    f_cols = pl.ds(pl.multiple_of(me * wub.shape[1], wub.shape[1]), wub.shape[1])
    wu_copy = fetch(wu_hbm.at[:, f_cols], wub)
    wd_copy = fetch(wd_hbm.at[:, o_cols], wdb)

    def sp_peer(off):
        return lax.rem(me + off, n_sp)

    def tp_peer(off):
        return lax.rem(my_tp + off, n_tp)

    grid_rel[...] = jnp.zeros_like(grid_rel)

    barrier = pltpu.get_barrier_semaphore()
    for off in range(1, n_sp):
        pl.semaphore_signal(barrier, inc=1, device_id={'sp': sp_peer(off)}, device_id_type=pl.DeviceIdType.MESH)
    for off in range(1, n_tp):
        pl.semaphore_signal(barrier, inc=1, device_id={'tp': tp_peer(off)}, device_id_type=pl.DeviceIdType.MESH)

    def remote(src, dst, send, recv, where):
        return pltpu.make_async_remote_copy(src_ref=src, dst_ref=dst, send_sem=send, recv_sem=recv, device_id=where,
                                            device_id_type=pl.DeviceIdType.MESH)

    sends = []

    def scatter(phase, src, dst):
        for off in range(1, n_sp):
            peer = sp_peer(off)
            copy = remote(src.at[peer], dst.at[me], ssem.at[phase, peer], rsem.at[phase, me], {'sp': peer})
            copy.start()
            sends.append(copy)

    def gather(phase, buf):
        for off in range(1, n_sp):
            peer = sp_peer(off)
            copy = remote(buf.at[me], buf.at[me], ssem.at[phase, peer], rsem.at[phase, me], {'sp': peer})
            copy.start()
            sends.append(copy)

    def arrived(phase, buf):
        for off in range(1, n_sp):
            peer = sp_peer(off)
            remote(buf.at[peer], buf.at[peer], ssem.at[phase, peer], rsem.at[phase, peer], {'sp': peer}).wait_recv()

    def tp_sum(phase, src, dst):
        dst[my_tp] = src[...]
        for off in range(1, n_tp):
            peer = tp_peer(off)
            copy = remote(src, dst.at[my_tp], tp_ssem.at[phase, peer], tp_rsem.at[phase, my_tp], {'tp': peer})
            copy.start()
            sends.append(copy)
        for off in range(1, n_tp):
            peer = tp_peer(off)
            remote(src, dst.at[peer], tp_ssem.at[phase, peer], tp_rsem.at[phase, peer], {'tp': peer}).wait_recv()
        total = dst[0]
        for t in range(1, n_tp):
            total = total + dst[t]
        return total

    wide = hid[...].astype(F32)
    inv = lax.rsqrt(jnp.mean(wide * wide, axis=-1, keepdims=True) + EPS)
    k_cols = pl.ds(pl.multiple_of(me * kk, kk), kk)
    normed = (hid[:, k_cols].astype(F32) * inv * ga[:, k_cols].astype(F32)).astype(BF16)

    spread = (lax.broadcasted_iota(jnp.int32, (LANES, LANES * heads), 1) // heads
              == lax.broadcasted_iota(jnp.int32, (LANES, LANES * heads), 0)).astype(F32).astype(BF16)
    wide_lane_head = lax.broadcasted_iota(jnp.int32, (batch, LANES * heads), 1) % heads
    lhs = []
    for c in range(kk // LANES):
        spread_in = jnp.dot(normed[:, c * LANES:(c + 1) * LANES], spread, preferred_element_type=F32)
        lhs.append(jnp.concatenate([jnp.where(wide_lane_head == h, spread_in, 0.0).astype(BF16) for h in range(heads)], axis=0))
    parts = []
    for i in range(3):
        w_copies[i].wait()
        acc = jnp.zeros((heads * batch, head_dim), F32)
        for c in range(kk // LANES):
            span = LANES * heads
            acc = acc + jnp.dot(lhs[c], wqkv[i, c * span:(c + 1) * span, :], preferred_element_type=F32)
        if i == 0:
            for h in range(heads):
                qsend[h] = acc[h * batch:(h + 1) * batch]
            pl.semaphore_wait(barrier, n_sp + n_tp - 2)
            scatter(0, qsend, qrecv)
            qrecv[me] = qsend[me]
        else:
            for h in range(heads):
                kvsend[h, i - 1] = acc[h * batch:(h + 1) * batch]
    scatter(1, kvsend, kvrecv)
    kvrecv[me] = kvsend[me]

    rel_copy.wait()
    group = 32

    def reverse(i, carry):
        tile = relb[pl.ds(pl.multiple_of(i * group, group), group)].astype(F32)
        flipped = jnp.concatenate([tile[group - 1 - j:group - j] for j in range(group)], axis=0)
        flipped = flipped.reshape(group * heads, head_dim).astype(BF16)
        at = pl.multiple_of((seq_blk // group - 1 - i) * group * heads, group * heads)
        rrev[pl.ds(at, group * heads), :] = flipped
        return carry

    lax.fori_loop(0, seq_blk // group, reverse, 0)

    arrived(0, qrecv)
    q_head = qrecv[0]
    for p in range(1, n_sp):
        q_head = q_head + qrecv[p]
    qall[me] = q_head.astype(BF16).astype(F32)
    gather(2, qall)
    arrived(2, qall)

    u_wide, w_wide = u_ref[...].astype(F32), w_ref[...].astype(F32)
    q_pos = jnp.concatenate([(qall[h] + w_wide[h:h + 1]).astype(BF16) for h in range(heads)], axis=0)
    lane_head = lax.broadcasted_iota(jnp.int32, (batch, LANES), 1) % heads

    def relative(c, carry):
        span = 2 * LANES
        table = rrev[pl.ds(pl.multiple_of(c * span, span), span), :]
        by_head = lax.dot_general(q_pos, table, NT, preferred_element_type=F32)
        for t in range(2):
            tile = by_head[:, t * LANES:(t + 1) * LANES]
            row = tile[:batch]
            for h in range(1, heads):
                row = jnp.where(lane_head == h, tile[h * batch:(h + 1) * batch], row)
            relsend[:, pl.ds(2 * c + t, 1), :] = row.reshape(batch, 1, LANES)
        return carry

    lax.fori_loop(0, rows // (2 * LANES), relative, 0)

    def rel_slot(src, dst):
        return grid_rel.at[:, pl.ds(pl.multiple_of((n_sp - 1 - src - dst) * rel_rows, rel_rows), rel_rows), :]

    for off in range(1, n_sp):
        peer = sp_peer(off)

        @pl.when(peer + me <= n_sp - 1)
        def _():
            remote(relsend, rel_slot(me, peer), rel_ssem.at[peer], rel_rsem.at[me], {'sp': peer}).start()

    @pl.when(me + me <= n_sp - 1)
    def _():
        at = pl.multiple_of((n_sp - 1 - me - me) * rel_rows, rel_rows)
        grid_rel[:, pl.ds(at, rel_rows), :] = relsend[...]

    for h in range(heads):
        qcb[:, h:h + 1, :] = (qall[h] + u_wide[h:h + 1]).reshape(batch, 1, head_dim)

    def wait_for(copy_src, copy_dst, b, first):
        pltpu.make_async_copy(copy_src.at[b], copy_dst.at[b], hsem.at[first + b]).wait()

    def content(b, carry):
        wait_for(k_hbm, kb, b, 4)
        q = qcb[b]
        zero = jnp.zeros_like(q)
        two = jnp.concatenate([jnp.concatenate([q, zero], axis=1), jnp.concatenate([zero, q], axis=1)], axis=0).astype(BF16)
        for c in range(half // 256):
            keys = jnp.concatenate([kb[b, c * 256:(c + 1) * 256, :], kb[b, half + c * 256:half + (c + 1) * 256, :]], axis=1)
            sc[b, :, c * 256:(c + 1) * 256] = lax.dot_general(two, keys, NT, preferred_element_type=F32)
        return carry

    lax.fori_loop(0, batch, content, 0)

    for off in range(1, n_sp):
        peer = sp_peer(off)

        @pl.when(peer + me <= n_sp - 1)
        def _():
            remote(relsend, rel_slot(peer, me), rel_ssem.at[peer], rel_rsem.at[peer], {'sp': peer}).wait_recv()

    r_iota = lax.broadcasted_iota(jnp.int32, (2 * heads, LANES), 0)
    l_iota = lax.broadcasted_iota(jnp.int32, (2 * heads, LANES), 1)
    slot = me * seq_blk + (r_iota // heads) * (seq_blk // 2) + l_iota // heads
    slot = jnp.where(r_iota % heads == l_iota % heads, slot, jnp.int32(2 ** 30))
    lane_row = lax.broadcasted_iota(jnp.int32, (rel_rows, LANES), 1)
    first_stat = lax.broadcasted_iota(jnp.int32, (heads, LANES), 1) < LANES // 2
    tiles = half // LANES

    def attend(b, carry):
        n = lens[b]
        start = smax - 1 - n
        row0 = jnp.minimum(start // per_row, (n_sp - 1) * rel_rows)
        turn = LANES - heads * (start % per_row)
        now = pltpu.roll(grid_rel[b, pl.ds(row0, rel_rows), :], turn, 1)
        after = pltpu.roll(grid_rel[b, pl.ds(row0 + 1, rel_rows), :], turn, 1)
        win[b] = jnp.where(lane_row < turn, now, after)
        wait_for(v_hbm, vb, b, 4 + batch)
        scores = []
        for c in range(tiles):
            rel = jnp.concatenate([jnp.broadcast_to(win[b, c:c + 1, :], (heads, LANES)),
                                   jnp.broadcast_to(win[b, tiles + c:tiles + c + 1, :], (heads, LANES))], axis=0)
            s = (sc[b, :, c * LANES:(c + 1) * LANES] + rel) * scale
            scores.append(jnp.where(slot < n - c * per_row, s, MASKED))
        top = functools.reduce(jnp.maximum, scores)
        top = jnp.max(top, axis=1, keepdims=True)
        top = jnp.maximum(jnp.maximum(top[:heads], top[heads:]), FLOOR)
        top2 = jnp.concatenate([top, top], axis=0)
        weights = [jnp.exp(s - top2) for s in scores]
        total = jnp.sum(functools.reduce(jnp.add, weights), axis=1, keepdims=True)
        total = total[:heads] + total[heads:]
        acc = jnp.zeros((2 * heads, 2 * head_dim), F32)
        for c in range(half // 256):
            values = jnp.concatenate([vb[b, c * 256:(c + 1) * 256, :], vb[b, half + c * 256:half + (c + 1) * 256, :]], axis=1)
            p = jnp.concatenate([weights[2 * c], weights[2 * c + 1]], axis=1).astype(BF16)
            acc = acc + jnp.dot(p, values, preferred_element_type=F32)
        ctx = acc[:heads, :head_dim] + acc[heads:, head_dim:]
        csend[:, 0, pl.ds(b, 1), :] = ctx.reshape(heads, 1, head_dim)
        stats = jnp.where(first_stat, top, total)
        csend[:, 1, pl.ds(b, 1), :] = stats.reshape(heads, 1, LANES)
        return carry

    lax.fori_loop(0, batch, attend, 0)

    scatter(3, csend, crecv)
    crecv[me] = csend[me]

    arrived(1, kvrecv)
    k_new, v_new = kvrecv[0, 0], kvrecv[0, 1]
    for p in range(1, n_sp):
        k_new, v_new = k_new + kvrecv[p, 0], v_new + kvrecv[p, 1]
    k_new = k_new.astype(BF16).astype(F32)
    v_new = v_new.astype(BF16).astype(F32)
    q_cont = (qall[me] + jnp.sum(jnp.where(lax.broadcasted_iota(jnp.int32, (heads, head_dim), 0) == me, u_wide, 0.0), axis=0, keepdims=True))
    q_cont = q_cont.astype(BF16).astype(F32)
    last_row = (n_sp - 1 - me) * rel_rows + rel_rows - 1
    zero_dist = grid_rel[:, pl.ds(last_row, 1), :].reshape(batch, LANES)
    lane_b = lax.broadcasted_iota(jnp.int32, (batch, LANES), 1)
    rel0 = jnp.sum(jnp.where(lane_b == LANES - heads + me, zero_dist, 0.0), axis=1, keepdims=True)
    s_new = (jnp.sum(q_cont * k_new, axis=1, keepdims=True) + rel0) * scale

    arrived(3, crecv)
    tops = [crecv[p, 1][:, :1] for p in range(n_sp)]
    sums = [crecv[p, 1][:, LANES - 1:] for p in range(n_sp)]
    best = functools.reduce(jnp.maximum, tops, s_new)
    e_new = jnp.exp(s_new - best)
    denom = e_new
    numer = e_new.astype(BF16).astype(F32) * v_new
    for p in range(n_sp):
        factor = jnp.exp(tops[p] - best)
        denom = denom + factor * sums[p]
        numer = numer + factor * crecv[p, 0]
    call[me] = (numer / denom).astype(BF16).astype(F32)
    gather(4, call)
    arrived(4, call)

    ctx_all = jnp.concatenate([call[h].astype(BF16) for h in range(heads)], axis=1)
    wo_copy.wait()
    aosend[...] = jnp.dot(ctx_all, wob[...], preferred_element_type=F32)
    attn = tp_sum(0, aosend, aorecv)
    x1 = (hid[:, o_cols].astype(F32) + attn).astype(BF16).astype(F32)
    x1all[me] = x1
    gather(5, x1all)
    arrived(5, x1all)

    x1_parts = [x1all[p] for p in range(n_sp)]
    mean_sq = functools.reduce(jnp.add, [jnp.sum(t * t, axis=-1, keepdims=True) for t in x1_parts]) / (co * n_sp)
    inv = lax.rsqrt(mean_sq + EPS)
    normed = jnp.concatenate([(t * inv * gm[:, p * co:(p + 1) * co].astype(F32)).astype(BF16) for p, t in enumerate(x1_parts)], axis=1)
    wu_copy.wait()
    up = jnp.dot(normed, wub[...], preferred_element_type=F32)
    aall[me] = jax.nn.gelu(up, approximate=True).astype(BF16).astype(F32)
    gather(6, aall)
    arrived(6, aall)
    act = jnp.concatenate([aall[p].astype(BF16) for p in range(n_sp)], axis=1)
    wd_copy.wait()
    dnsend[...] = jnp.dot(act, wdb[...], preferred_element_type=F32)
    down = tp_sum(1, dnsend, dnrecv)
    oall[me] = (x1all[me] + down).astype(BF16).astype(F32)
    gather(7, oall)
    arrived(7, oall)
    for p in range(n_sp):
        out_ref[:, p * co:(p + 1) * co] = oall[p].astype(BF16)

    for copy in sends:
        copy.wait_send()
    for off in range(1, n_sp):
        peer = sp_peer(off)

        @pl.when(peer + me <= n_sp - 1)
        def _():
            remote(relsend, rel_slot(me, peer), rel_ssem.at[peer], rel_rsem.at[me], {'sp': peer}).wait_send()


def solution(mesh):
    n_sp, n_tp = mesh.shape['sp'], mesh.shape['tp']
    spec_rows = P('dp', None)
    spec_cache = P('dp', 'sp', 'tp', None)
    in_specs = (spec_rows, spec_cache, spec_cache, P('dp'), P('sp', 'tp', None), P('tp', None), P('tp', None), P(None), P(None, 'tp', None), P(None, 'tp', None), P(None, 'tp', None), P('tp', None, None), P(None), P(None, 'tp'), P('tp', None))
    out_specs = spec_rows

    def layer_step(hidden, k_cache, v_cache, lengths, rel_table, u_bias, w_bias, g_attn, w_query, w_key, w_value, w_out, g_mlp, w_up, w_down):
        batch, seq_blk, heads, head_dim = k_cache.shape
        width = hidden.shape[1]
        ff = w_up.shape[1]
        rows = seq_blk * heads
        kk = width // n_sp
        co = width // n_sp
        cf = ff // n_sp
        rel_rows = rows // LANES
        vmem = functools.partial(pl.BlockSpec, memory_space=pltpu.VMEM)
        hbm = functools.partial(pl.BlockSpec, memory_space=pl.ANY)
        dma = pltpu.SemaphoreType.DMA
        phases = 8
        return pl.pallas_call(
            functools.partial(layer_kernel, n_sp, n_tp),
            out_shape=jax.ShapeDtypeStruct((batch, width), BF16),
            in_specs=[pl.BlockSpec(memory_space=pltpu.SMEM)] + [vmem()] * 5 + [hbm()] * 9,
            out_specs=vmem(),
            scratch_shapes=[
                pltpu.VMEM((3, kk * heads, head_dim), BF16),
                pltpu.VMEM((seq_blk, heads, head_dim), BF16),
                pltpu.VMEM((rows, head_dim), BF16),
                pltpu.VMEM((batch, rows, head_dim), BF16),
                pltpu.VMEM((batch, rows, head_dim), BF16),
                pltpu.VMEM((heads * head_dim, co), BF16),
                pltpu.VMEM((width, cf), BF16),
                pltpu.VMEM((ff, co), BF16),
                pltpu.VMEM((n_sp, batch, head_dim), F32),
                pltpu.VMEM((n_sp, batch, head_dim), F32),
                pltpu.VMEM((n_sp, 2, batch, head_dim), F32),
                pltpu.VMEM((n_sp, 2, batch, head_dim), F32),
                pltpu.VMEM((n_sp, batch, head_dim), F32),
                pltpu.VMEM((batch, heads, head_dim), F32),
                pltpu.VMEM((batch, rel_rows, LANES), F32),
                pltpu.VMEM((batch, n_sp * rel_rows + 8, LANES), F32),
                pltpu.VMEM((batch, rel_rows, LANES), F32),
                pltpu.VMEM((batch, 2 * heads, rows // 2), F32),
                pltpu.VMEM((n_sp, 2, batch, head_dim), F32),
                pltpu.VMEM((n_sp, 2, batch, head_dim), F32),
                pltpu.VMEM((n_sp, batch, head_dim), F32),
                pltpu.VMEM((batch, co), F32),
                pltpu.VMEM((n_tp, batch, co), F32),
                pltpu.VMEM((n_sp, batch, co), F32),
                pltpu.VMEM((n_sp, batch, cf), F32),
                pltpu.VMEM((batch, co), F32),
                pltpu.VMEM((n_tp, batch, co), F32),
                pltpu.VMEM((n_sp, batch, co), F32),
                dma((7 + 2 * batch,)),
                dma((phases, n_sp)),
                dma((phases, n_sp)),
                dma((n_sp,)),
                dma((n_sp,)),
                dma((2, n_tp)),
                dma((2, n_tp)),
            ],
            compiler_params=pltpu.CompilerParams(collective_id=0, has_side_effects=True, vmem_limit_bytes=67043328),
            name='decode_layer',
        )(lengths, hidden, u_bias, w_bias, g_attn.reshape(1, width), g_mlp.reshape(1, width), rel_table,
          k_cache.reshape(batch, rows, head_dim), v_cache.reshape(batch, rows, head_dim),
          w_query.reshape(width * heads, head_dim), w_key.reshape(width * heads, head_dim), w_value.reshape(width * heads, head_dim),
          w_out.reshape(heads * head_dim, width), w_up, w_down)

    return jax.shard_map(layer_step, mesh=mesh, in_specs=in_specs, out_specs=out_specs, check_vma=False)
```

time: 290 us -> 90.2 us (0.31)
  Pallas kernels: 0 us -> 85.8 us
  waiting for transfers between devices: 78.1 us -> 0 us
  other arithmetic: 67.9 us -> 0 us
  matrix products: 53.1 us -> 0 us
  local copies, waits for them, and re-layouts: 54.1 us -> 4.18 us
  blocking collectives: 21.7 us -> 0 us
  between operations: 13.3 us -> 0.01 us
    pallas_call x0 -> x1, Pallas kernels: none -> 85.8 us  [layer_step(): pl.pallas_call(functools.partial(layer_kernel, n_sp, n_tp), out_shape=jax...]
    psum x2 -> x0, waiting for transfers between devices: 78 us -> none  [the longest x1 40.6 us: layer_step(): attn_out = lax.psum(attn_part, 'tp')]
    dot_general x7 -> x0, matrix products: 53.1 us -> none  [the longest x1 24.7 us: layer_step(): down_part = jnp.dot(activated, w_down, preferred_element_type=jnp.float32)]
    unnamed x1 -> x0, other arithmetic: 29 us -> none
    pad x1 -> x0, local copies, waits for them, and re-layouts: 25.2 us -> none  [distance_to_position(): padded = jnp.pad(by_distance, ((0, 0), (0, 0), (width, 0)))]
    all_gather x1 -> x0, blocking collectives: 21.7 us -> none  [layer_step(): gathered = lax.all_gather(packed, 'sp', axis=0)]
    unnamed x18 -> x1, local copies, waits for them, and re-layouts: 18.1 us -> 1.57 us
    convert_element_type x7 -> x0, other arithmetic: 14.3 us -> none  [the longest x1 10.4 us: layer_step(): weights.astype(jnp.bfloat16)]
  transfers between devices with their start and end apart: 3 -> 0, of which waited for: 2 -> 0; matrix products, arithmetic and copies ran while one was open for 18% -> 0% of each run, Pallas kernels for 0% -> 0%
where the time goes in v1:
time: 90.2 us; the launch traced here: 90 us
  Pallas kernels  85.8 us (95%)
  local copies, waits for them, and re-layouts  4.18 us (5%)
    pallas_call x1, Pallas kernels, layer_step(): pl.pallas_call(functools.partial(layer_kernel, n_sp, n_tp), out_shape=jax...  85.8 us

profile of v1, /device:TPU:97, one launch (start us, length us, event | category | flops | bytes accessed | tf_op | source)
XLA Modules:
  0.0 90.0 jit_solution(14850735200201941541)
XLA Ops:
  0.0 1.3 %reshape.24.ga = bf16[1,4096]{1,0:T(2,128)(2,1)} reshape(bf16[4096]{0:T(1024)(128)(2,1)} %param.22) | data formatting | bytes 16384 | tf_op jit(solution)/shard_map/reshape | solution.py:401
  1.3 1.3 %reshape.25.gm = bf16[1,4096]{1,0:T(2,128)(2,1)} reshape(bf16[4096]{0:T(1024)(128)(2,1)} %param.27) | data formatting | bytes 16384 | tf_op jit(solution)/shard_map/reshape | solution.py:401
  2.6 85.8 %decode_layer.1 = bf16[16,4096]{1,0:T(8,128)(2,1)} custom-call(s32[16]{0:T(128)} %lens.1, bf16[16,4096]{1,0:T(8,128)(2,1)} %hid.1, bf16[8,128]{1,0:T(8,128)(2,1)} %u_ref.1, bf16[8,128]{1,0:T(8,128)(2,1)} %w_ref.1, bf16[1,4096]{1,0:T(2,128)(2,1)} %reshape.24.ga, bf16[1,4096]{1,0:T(2,128)(2,1)} %reshape.25.gm, bf16[512,8,128]{2,1,0:T(8,128)(2,1)} %rel_hbm.1, ...), custom_call_target="tpu_custom_call" | custom-call | tf_op jit(solution)/shard_map/decode_layer/pallas_call | solution.py:357
  88.4 1.6 %copy.17 = bf16[16,4096]{1,0:T(8,128)(2,1)} copy(bf16[16,4096]{1,0:T(8,128)(2,1)} %decode_layer.1) | data formatting | bytes 262144
